TPU v7x, 32 devices: a whole 2x2x4 slice. The times are simulated.
32 devices in a mesh: gx: 8 (over y, x, core), gy: 4 (over z).
Axes of the slice: x: 2, y: 2, z: 4, core: 2. Of those that a mesh axis runs over, the one named last changes fastest.
Arguments:
- ocean_heat_field: float32 [8, 192, 128, 128], P('gy', 'gx'), may hold values from -6 to 6
- patch_zone: int32 [192], replicated, may hold values from 0 to 31, as said below
- patch_position: int32 [192], replicated, may hold values from 0 to 11, as said below
- quarter_spins: int32 [192], replicated, may hold values from 0 to 3
- zone_patch_tally: int32 [32], P(('gx', 'gy')), may hold values from 0 to 12, as said below
Outputs:
- regional: float32 [8, 32, 12, 128, 128], P(None, ('gx', 'gy'))
Inputs may be any that keep to these rules, and one draw needn't show every extreme that they name: In each aligned group of 24 blocks no more than 6 go to regions of one column patch_zone // 4, and each group has a column with exactly 6. A region receives at most 12 blocks and some region receives exactly 12. `patch_position`: the blocks of one region have distinct slots 0 to zone_patch_tally of that region minus 1, in increasing block order. zone_patch_tally[r] is the number of blocks j with patch_zone[j] = r.
All inputs are finite; a program needn't handle non-finite values.
Results may differ from a plain program's by a relative error of at most 0.00002.
Values sent between devices are 32-bit elements; how exact they have to be, the bound alone decides.
A program may use at most 128 MiB of HBM per device.

v0:
```python
import functools

import jax
import jax.numpy as jnp
from jax import lax
from jax.experimental import pallas as pl
from jax.experimental.pallas import tpu as pltpu
from jax.sharding import PartitionSpec as P

MESH = pl.DeviceIdType.MESH
PART = 8
STEP_BLOCKS = 4
VMEM_BYTES = 52 * 2**20


def chunk_units(times, side):
    units = [(r, t) for r in range(side // (2 * PART)) for t in range(times)]
    small = 2 * (times // 2 + times % 2)
    cuts = list(range(0, small + 1, max(times // 2, 1)))
    cuts += list(range(small + times, len(units) - small + 1, times))
    cuts += list(range(len(units) - small + max(times // 2, 1), len(units) + 1, max(times // 2, 1)))
    return [units[a:b] for a, b in zip(cuts[:-1], cuts[1:])]


def time_major(times, side):
    units = [(r, t) for t in range(times) for r in range(side // (2 * PART))]
    sizes = [1, 1] + [2] * ((len(units) - 4) // 2) + [1, 1]
    cuts = [sum(sizes[:c]) for c in range(len(sizes) + 1)]
    return [units[a:b] for a, b in zip(cuts[:-1], cuts[1:])]


def mirror_lanes(block):
    side = block.shape[1]
    lane = side - 1 - lax.broadcasted_iota(jnp.int32, block.shape, 1)
    return jnp.take_along_axis(block, lane, axis=1)


def turn_blocks(first, chunks, spins, field, turned):
    times, blocks, side, _ = field.shape
    for b in range(blocks):
        code = spins[first + b]
        for kind in range(4):
            @pl.when(code == kind)
            def _(kind=kind, b=b):
                for t in range(times):
                    block = field[t, b]
                    if kind == 1:
                        block = mirror_lanes(block).T
                    elif kind == 2:
                        block = mirror_lanes(mirror_lanes(block).T).T
                    elif kind == 3:
                        block = mirror_lanes(block.T)
                    for c, chunk in enumerate(chunks):
                        for i, (r, at) in enumerate(chunk):
                            if at == t:
                                for h in range(2):
                                    top = h * (side // 2) + r * PART
                                    turned[c][h, b, i] = block[top:top + PART]


def prepare(dims, zone, slot, spins, field, *refs):
    pairs, rows, per_group, per_pair, cap, chunks, sizes = dims
    turned = refs[:len(chunks)]
    send_table, pick_table, tallies, choice, counts, fills = refs[len(chunks):]
    gx = lax.axis_index("gx")
    pair = gx // 2
    group = 2 * per_group
    local = 2 * rows
    step = pl.program_id(0)

    @pl.when(step == 0)
    def _():
        def clear(ref, size):
            def body(i, c):
                ref[i] = 0
                return c
            lax.fori_loop(0, size, body, 0, unroll=8)
        clear(send_table, pairs * per_pair + 1)
        clear(pick_table, local * cap + 1)
        clear(counts, pairs * local)
        clear(fills, pairs * pairs)

        for source in range(pairs):
            behind = lax.rem(pair - source + pairs, pairs) * per_pair

            def place(j, c, source=source, behind=behind):
                region = zone[source * group + j]
                counts[region] = counts[region] + 1
                target = region // local
                cell = source * pairs + target
                rank = fills[cell]
                fills[cell] = rank + 1
                ahead = lax.rem(target - source + pairs, pairs) * per_pair
                send_table[jnp.where(source == pair, ahead + rank, pairs * per_pair)] = j
                at = (region - target * local) * cap + slot[source * group + j]
                pick_table[jnp.where(target == pair, at, local * cap)] = behind + rank
                return c
            lax.fori_loop(0, group, place, 0, unroll=4)
        most_pair = jnp.int32(0)
        most_row = jnp.int32(0)
        for q in range(pairs):
            for r in range(pairs):
                if q != r:
                    most_pair = jnp.maximum(most_pair, fills[q * pairs + r])
            pooled = [counts[q * local + r] + counts[q * local + rows + r] for r in range(rows)]
            for value in pooled:
                most_row = jnp.maximum(most_row, value)
        for r in range(local):
            tallies[r] = counts[pair * local + r]
        chosen = jnp.int32(len(sizes) - 1)
        for at in range(len(sizes) - 2, -1, -1):
            wide, tall = sizes[at]
            fits = jnp.logical_and(most_pair <= wide, most_row <= tall)
            chosen = jnp.where(fits, at, chosen)
        choice[0] = chosen

    turn_blocks(gx * per_group + step * field.shape[1], chunks, spins, field, turned)


def origin_of(z, rows, k, relay):
    if not relay:
        return lax.rem(z - k + rows, rows)
    low = z < 2
    return [z, z + 1 - 2 * lax.rem(z, 2), jnp.where(low, 2, 1), jnp.where(low, 3, 0)][k]


def exchange(dims, send_table, pick_table, tallies, *refs):
    pairs, rows, per_group, per_pair, wide, tall, cap, chunks = dims
    turned, final, scratch = refs[:chunks], refs[chunks:2 * chunks], refs[2 * chunks:]
    kinds = 7
    groups = [scratch[i * chunks:(i + 1) * chunks] for i in range(kinds)]
    held, packed, landed, lifted, risen, given, kept = groups
    sems = list(scratch[kinds * chunks:])
    row_list = sems.pop(0)
    own_sem, swap_send, swap_recv, pair_send, pair_recv, row_send, row_recv, give_send, give_recv, keep_sem = sems
    gx = lax.axis_index("gx")
    z = lax.axis_index("gy")
    pair = gx // 2
    half = lax.rem(gx, 2)
    mate = (2 * pair + 1 - half, z)

    def across(o):
        return (2 * lax.rem(pair + o, pairs) + half, z)

    def along(o):
        return (gx, lax.rem(z + o, rows))

    barrier = pltpu.get_barrier_semaphore()
    friends = [mate] + [across(o) for o in range(1, pairs)] + [along(o) for o in range(1, rows)]
    for friend in friends:
        pl.semaphore_signal(barrier, inc=1, device_id=friend, device_id_type=MESH)
    own_copies = []
    for c in range(chunks):
        own = pltpu.make_async_copy(turned[c].at[half], held[c].at[pl.ds(half * per_group, per_group)], own_sem.at[c])
        own.start()
        own_copies.append(own)
    pl.semaphore_wait(barrier, len(friends))

    swaps = []
    for c in range(chunks):
        swap = pltpu.make_async_remote_copy(
            src_ref=turned[c].at[1 - half], dst_ref=held[c].at[pl.ds(half * per_group, per_group)],
            send_sem=swap_send.at[c], recv_sem=swap_recv.at[c], device_id=mate, device_id_type=MESH)
        swap.start()
        swaps.append(swap)

    unsent = []
    pair_copies = []
    for c in range(chunks):
        own_copies[c].wait()
        swaps[c].wait_recv()
        unsent.append(swaps[c])
        sent = []
        for o in range(1, pairs):
            def pack(k, carry, o=o, c=c):
                packed[c][o - 1, k] = held[c][send_table[o * per_pair + k]]
                return carry
            lax.fori_loop(0, wide, pack, 0, unroll=4)
            copy = pltpu.make_async_remote_copy(
                src_ref=packed[c].at[o - 1], dst_ref=landed[c].at[pl.ds(o * per_pair, wide)],
                send_sem=pair_send.at[c, o - 1], recv_sem=pair_recv.at[c, o - 1],
                device_id=across(o), device_id_type=MESH)
            copy.start()
            sent.append(copy)
        unsent.extend(sent)

        def stay(k, carry, c=c):
            landed[c][k] = held[c][send_table[k]]
            return carry
        lax.fori_loop(0, per_pair, stay, 0, unroll=4)
        pair_copies.append(sent)

    for r in range(rows):
        first = tallies[r]

        def compact(k, carry, r=r, first=first):
            at = jnp.minimum(jnp.where(k < first, r * cap + k, (rows + r) * cap + k - first), 2 * rows * cap - 1)
            row_list[r * tall + k] = pick_table[at]
            return carry
        lax.fori_loop(0, tall, compact, 0, unroll=4)

    gives = []

    def settle_all(c):
        first = tallies[z]

        def settle(s, carry, c=c):
            mine = jnp.minimum(s + half * first, tall - 1)
            other = jnp.minimum(s + (1 - half) * first, tall - 1)
            for o in range(rows):
                given[c][s, o] = risen[c][o, other]
                kept[c][s, o] = risen[c][o, mine]
            return carry
        lax.fori_loop(0, cap, settle, 0)
        give = pltpu.make_async_remote_copy(
            src_ref=given[c], dst_ref=final[c].at[half],
            send_sem=give_send.at[c], recv_sem=give_recv.at[c], device_id=mate, device_id_type=MESH)
        give.start()
        keep = pltpu.make_async_copy(kept[c], final[c].at[half], keep_sem.at[c])
        keep.start()
        gives.append((give, keep))

    row_copies = []
    for c in range(chunks):
        for copy in pair_copies[c]:
            copy.wait_recv()
        sent = []
        for o in list(range(rows - 1, 0, -1)) + [0]:
            row = lax.rem(z + o, rows)

            def lift(k, carry, o=o, c=c, row=row):
                tile = landed[c][row_list[row * tall + k]]
                if o > 0:
                    lifted[c][o - 1, k] = tile
                else:
                    risen[c][0, k] = tile
                return carry
            lax.fori_loop(0, tall, lift, 0, unroll=4)
            if o > 0:
                copy = pltpu.make_async_remote_copy(
                    src_ref=lifted[c].at[o - 1], dst_ref=risen[c].at[o],
                    send_sem=row_send.at[c, o - 1], recv_sem=row_recv.at[c, o - 1],
                    device_id=along(o), device_id_type=MESH)
                copy.start()
                sent.append(copy)
        row_copies.append(sent)
        unsent.extend(sent)
    for c in range(chunks):
        for copy in row_copies[c]:
            copy.wait_recv()
        settle_all(c)
    for copy in unsent:
        copy.wait_send()
    for give, keep in gives:
        give.wait()
        keep.wait()


def finish(rows, chunks, tally, *refs):
    final, regional = refs[:-1], refs[-1]
    z = lax.axis_index("gy")
    slot = pl.program_id(0)
    side = regional.shape[3]
    times = regional.shape[0] // rows
    place = {unit: (c, i) for c, chunk in enumerate(chunks) for i, unit in enumerate(chunk)}

    @pl.when(slot < tally[0])
    def _():
        for h in range(2):
            for r in range(side // (2 * PART)):
                span = pl.ds(h * (side // 2) + r * PART, PART)
                tiles = {}
                for t in range(times):
                    c, i = place[(r, t)]
                    for o in range(rows):
                        tiles[o, t] = final[c][h, 0, o, i]
                mean = sum(tiles.values()) * jnp.float32(1.0 / (rows * times))
                for o in range(rows):
                    start = origin_of(z, rows, o, False) * times
                    for t in range(times):
                        regional[start + t, 0, 0, span, :] = tiles[o, t] - mean

    @pl.when(slot >= tally[0])
    def _():
        regional[...] = jnp.zeros_like(regional)


def levels(most, steps):
    return sorted({-(-most * s // 48) for s in steps})


def balanced_sizes(per_pair, tall):
    steps = ((38, 34, 52), (38, 36, 54), (40, 36, 56), (40, 38, 58), (42, 40, 60), (48, 46, 68), (48, 48, 96))
    return [(-(-per_pair * w // 48), -(-tall * e // 48), -(-tall * f // 48)) for w, e, f in steps]

def beside(x, step):
    return jnp.concatenate([x[step:], x[:step]], axis=0)


def plan_tables(dims, sizes, pair, zone, slot, allow):
    pairs, rows, per_group, per_pair, cap, extra = dims
    group, local, tall = 2 * per_group, 2 * rows, 2 * cap
    bins = pairs * rows
    width = zone.shape[1]
    i32, f32, bf16 = jnp.int32, jnp.float32, jnp.bfloat16
    lane = lax.broadcasted_iota(i32, (1, width), 1)
    valid = zone >= 0
    source = sum((lane >= group * k).astype(i32) for k in range(1, pairs))
    home = sum((zone >= local * k).astype(i32) for k in range(1, pairs))
    inside = zone - home * local
    side = (inside >= rows).astype(i32)
    row = inside - side * rows
    bin_at = lax.broadcasted_iota(i32, (bins, width), 0)
    before = (lax.broadcasted_iota(i32, (width, width), 0) < lax.broadcasted_iota(i32, (width, width), 1)).astype(bf16)

    def marks(key):
        return jnp.where(bin_at == jnp.where(valid, key, -1), 1.0, 0.0).astype(f32)

    def tally(mark):
        return jnp.sum(mark, axis=1, keepdims=True)

    def look(mark, table):
        return jnp.sum(mark * table, axis=0, keepdims=True)

    def ranks(mark):
        return jnp.dot(mark.astype(bf16), before, preferred_element_type=f32)

    at = lax.broadcasted_iota(i32, (bins, 128), 0)
    at_row = at & (rows - 1)
    at_home = at >> (rows.bit_length() - 1)
    edge = jnp.logical_or(at_row == 0, at_row == rows - 1)

    def flip(x, bit):
        step = 1 << bit
        if 2 * step == bins:
            return beside(x, step)
        return jnp.where((at & step) == 0, beside(x, step), beside(x, bins - step))

    across_x = lambda x: flip(x, 2)
    across_y = lambda x: flip(x, 3)
    mark = marks(home * rows + row)
    order = look(mark, ranks(mark))
    native = jnp.broadcast_to(tally(mark), (bins, 128)).astype(i32)

    def whole(x):
        x = x + across_x(x)
        return x + across_y(x)

    load = native
    half_sum = whole(native + flip(native, 0))
    goal = (jnp.maximum(half_sum, flip(half_sum, 1)) + pairs - 1) >> (pairs.bit_length() - 1)
    row_sum = (whole(native) + pairs - 1) >> (pairs.bit_length() - 1)
    end_goal = jnp.maximum(jnp.maximum(row_sum, flip(flip(row_sum, 0), 1)), (9 * goal) >> 4)
    used = [jnp.zeros_like(native), jnp.zeros_like(native)]
    for _ in range(2):
        for d, partner in enumerate((across_x, across_y)):
            for stage in range(3):
                now, want = (load, end_goal) if stage == 0 else (load + flip(load, 0), goal)
                here = jnp.logical_not(edge) if stage == 1 else edge
                move = jnp.minimum((now - partner(now)) >> 1, now - want)
                move = jnp.minimum(move, jnp.minimum(extra - used[d], native - used[0] - used[1]))
                move = jnp.where(here, jnp.maximum(move, 0), 0)
                used[d] = used[d] + move
                load = load + partner(move) - move
    first = look(mark, (used[0] * allow)[:, :1].astype(f32))
    second = look(mark, (used[1] * allow)[:, :1].astype(f32))
    leaves_x = order < first
    leaves_y = jnp.logical_and(order >= first, order < first + second)
    way = leaves_y.astype(i32)
    guest = order - jnp.where(leaves_y, first, 0.0)
    home_x = home & 1
    home_y = home >> 1
    via = jnp.where(leaves_x, home_y * 2 + 1 - home_x, jnp.where(leaves_y, (1 - home_y) * 2 + home_x, home))

    flow = marks(source * pairs + via)
    line = marks(via * rows + row)
    both = ranks(jnp.concatenate([flow, line], axis=0))
    rank = look(flow, both[:bins])
    place = look(line, both[bins:])
    flows = jnp.broadcast_to(tally(flow), (bins, 128))
    lines = jnp.broadcast_to(tally(line), (bins, 128))
    halves = lines + flip(lines, 0)
    stays = at_home == at_row
    chosen = jnp.zeros((1, 128), f32)
    for wide, end, far in sizes:
        over = jnp.where(flows > jnp.where(stays, per_pair, wide).astype(f32), 1.0, 0.0)
        over = jnp.maximum(over, jnp.where(lines > jnp.where(edge, end, tall).astype(f32), 1.0, 0.0))
        over = jnp.maximum(over, jnp.where(halves > jnp.float32(far), 1.0, 0.0))
        chosen = chosen + jnp.max(over, axis=0, keepdims=True)

    my_x, my_y = pair % 2, pair // 2

    def offset(other):
        other_y = other >> 1
        other_x = other - 2 * other_y
        return jnp.where(other_x == my_x, 0, 1) + jnp.where(other_y == my_y, 0, 2)

    def invert(here, key, value):
        key = jnp.where(jnp.logical_and(valid, here), key, -1)
        hit = jnp.where(lax.broadcasted_iota(i32, (128, width), 0) == key, 1.0, 0.0).astype(bf16)
        value = jnp.broadcast_to(value.astype(bf16), (16, width))
        return lax.dot_general(value, hit, (((1,), (1,)), ((), ())), preferred_element_type=f32)[:1]

    rank = rank.astype(i32)
    place = place.astype(i32)
    guest = guest.astype(i32)
    landing = offset(source) * per_pair + rank
    mine = via == pair
    ours = home == pair
    return chosen, [
        invert(source == pair, offset(via) * per_pair + rank, (lane - group * pair).astype(f32)),
        invert(mine, row * tall + place, landing.astype(f32)),
        invert(jnp.logical_and(mine, home != pair), (way * rows + row) * extra + guest, place.astype(f32)),
        invert(ours, (side * rows + row) * cap + slot, jnp.where(mine, place, tall + way * extra + guest).astype(f32)),
        invert(mine, row, jnp.ones((1, width), f32)),
        invert(ours, side * rows + row, jnp.ones((1, width), f32)),
    ]


def prepare_balanced(dims, sizes, zone, slot, table, choice, padded):
    pair = lax.axis_index("gx") // 2
    padded[...] = jnp.full_like(padded, -1)
    padded[0:1, 0:zone.shape[1]] = zone[...]
    padded[1:2, 0:zone.shape[1]] = slot[...]

    def fill(sizes, allow):
        chosen, lines = plan_tables(dims, sizes, pair, padded[0:1], padded[1:2], allow)
        for k, line in enumerate(lines):
            table[k:k + 1] = line.astype(jnp.int32)
        return jnp.max(chosen).astype(jnp.int32)

    chosen = fill(sizes, 1)
    choice[0] = jnp.minimum(chosen, len(sizes) - 1)

    @pl.when(chosen == len(sizes))
    def _():
        fill(sizes[:0], 0)


def mirror_rows(block):
    side = block.shape[0]
    row = PART - 1 - lax.broadcasted_iota(jnp.int32, (PART, block.shape[1]), 0)
    parts = [block[r - PART:r] for r in range(side, 0, -PART)]
    return jnp.concatenate([jnp.take_along_axis(part, row, axis=0) for part in parts], axis=0)


def turn(block, code):
    block = jnp.where(jnp.logical_or(code == 1, code == 2), mirror_lanes(block), block)
    block = jnp.where(code >= 2, mirror_rows(block), block)
    return jnp.where(jnp.logical_or(code == 1, code == 3), block.T, block)


def exchange_balanced(dims, chunks, table, spins, field, regional, *scratch):
    pairs, rows, per_group, per_pair, cap, extra, wide, end, far = dims
    tall = 2 * cap
    count = len(chunks)
    times, _, side, _ = field.shape
    strips = side // (2 * PART)
    kinds = 12
    groups = [scratch[i * count:(i + 1) * count] for i in range(kinds)]
    held, swapped, packed, landed, lifted, risen, pooled, crossed_in, crossed_out, passed, leaving, visiting = groups
    crossed = (crossed_in, crossed_out)
    raw, given, far_list, *sems = scratch[kinds * count:]
    raw_sem, swap_send, swap_recv, pair_send, pair_recv, near_send, near_recv = sems[:7]
    give_send, give_recv, far_send, far_recv, pass_send, pass_recv, side_send, side_recv = sems[7:]
    unit_at = {unit: (c, i) for c, chunk in enumerate(chunks) for i, unit in enumerate(chunk)}
    gx = lax.axis_index("gx")
    z = lax.axis_index("gy")
    pair = gx // 2
    half = lax.rem(gx, 2)
    mate = (2 * pair + 1 - half, z)
    pair_x = lax.rem(pair, 2)
    pair_y = pair // 2
    near, far_in, far_out = (origin_of(z, rows, k, True) for k in (1, 2, 3))
    inner = jnp.logical_or(z == 1, z == 2)
    outer = jnp.logical_not(inner)

    def across(o):
        x = 1 - pair_x if o % 2 else pair_x
        y = 1 - pair_y if o // 2 else pair_y
        return (2 * (2 * y + x) + half, z)

    loads = []
    for t in range(times):
        loads.append(pltpu.make_async_copy(field.at[t], raw.at[pl.ds(t * per_group, per_group)], raw_sem.at[t]))
        loads[t].start()

    barrier = pltpu.get_barrier_semaphore()
    friends = [mate] + [across(o) for o in range(1, pairs)] + [(gx, lax.rem(z + o, rows)) for o in range(1, rows)]
    for friend in friends:
        pl.semaphore_signal(barrier, inc=1, device_id=friend, device_id_type=MESH)

    def turn_time(t):
        loads[t].wait()

        def one(b, carry):
            block = turn(raw[t * per_group + b], spins[gx * per_group + b])
            for r in range(strips):
                c, i = unit_at[r, t]
                top = block[r * PART:(r + 1) * PART]
                bottom = block[side // 2 + r * PART:side // 2 + (r + 1) * PART]
                held[c][half * per_group + b, i] = jnp.where(half == 0, top, bottom)
                swapped[c][b, i] = jnp.where(half == 0, bottom, top)
            return carry
        lax.fori_loop(0, per_group, one, 0, unroll=4)

    def wait_sent(sem, blocks):
        span = raw.at[pl.ds(0, blocks)]
        pltpu.make_async_copy(span, span, sem).wait()

    turn_time(0)
    pl.semaphore_wait(barrier, len(friends))

    swaps = {}

    def swap_time(t):
        for c in sorted({unit_at[r, t][0] for r in range(strips)}):
            swaps[c] = pltpu.make_async_remote_copy(
                src_ref=swapped[c], dst_ref=held[c].at[pl.ds(half * per_group, per_group)],
                send_sem=swap_send.at[0], recv_sem=swap_recv.at[c], device_id=mate, device_id_type=MESH)
            swaps[c].start()

    swap_time(0)

    def send_pairs(c):
        if c == 1:
            for t in range(1, times):
                turn_time(t)
                swap_time(t)
        swaps[c].wait_recv()
        sent = []
        for o in range(1, pairs):
            def pack(k, carry, o=o):
                packed[c][o - 1, k] = held[c][table[0, o * per_pair + k]]
                return carry
            lax.fori_loop(0, wide, pack, 0, unroll=4)
            sent.append(pltpu.make_async_remote_copy(
                src_ref=packed[c].at[o - 1], dst_ref=landed[c].at[pl.ds(o * per_pair, wide)],
                send_sem=pair_send.at[o - 1], recv_sem=pair_recv.at[c],
                device_id=across(o), device_id_type=MESH))

        @pl.when(half == 0)
        def _():
            for copy in sent:
                copy.start()

        @pl.when(half == 1)
        def _():
            for copy in sent[::-1]:
                copy.start()

        def stay(k, carry):
            landed[c][k] = held[c][table[0, k]]
            return carry
        lax.fori_loop(0, per_pair, stay, 0, unroll=4)

        if c == 0:
            lead = table[4, far_in]

            def gather_far(k, carry):
                at = jnp.where(k < lead, far_in * tall + k, far_out * tall + k - lead)
                far_list[k] = table[1, jnp.minimum(at, rows * tall - 1)]
                return carry
            lax.fori_loop(0, far, gather_far, 0, unroll=4)

    skip = table[4, z]

    def near_copy(c, size):
        return pltpu.make_async_remote_copy(
            src_ref=lifted[c].at[pl.ds(0, size)], dst_ref=risen[c].at[1, pl.ds(0, size)],
            send_sem=near_send.at[0], recv_sem=near_recv.at[c],
            device_id=(gx, near), device_id_type=MESH)

    def far_copy(c, place):
        return pltpu.make_async_remote_copy(
            src_ref=pooled[c], dst_ref=crossed[place][c],
            send_sem=far_send.at[0], recv_sem=far_recv.at[c, place],
            device_id=(gx, far_in), device_id_type=MESH)

    def pass_copy(c, place):
        return pltpu.make_async_remote_copy(
            src_ref=passed[c].at[place], dst_ref=risen[c].at[2 + place, pl.ds(0, end)],
            send_sem=pass_send.at[0], recv_sem=pass_recv.at[c],
            device_id=(gx, near), device_id_type=MESH)

    def side_copy(c, d):
        return pltpu.make_async_remote_copy(
            src_ref=leaving[c].at[d], dst_ref=visiting[c].at[d],
            send_sem=side_send.at[0], recv_sem=side_recv.at[c],
            device_id=across(1 + d), device_id_type=MESH)

    def send_rows(c):
        pltpu.make_async_copy(packed[c], packed[c], pair_recv.at[c]).wait()

        def pool(k, carry):
            pooled[c][k] = landed[c][far_list[k]]
            return carry
        lax.fori_loop(0, far, pool, 0, unroll=4)

        def lift(k, carry):
            lifted[c][k] = landed[c][table[1, near * tall + k]]
            return carry
        lax.fori_loop(0, tall, lift, 0, unroll=4)

        def send_far():
            for place, mine in enumerate((inner, outer)):
                @pl.when(mine)
                def _(place=place):
                    far_copy(c, place).start()

        @pl.when(half == 0)
        def _():
            send_far()

        @pl.when(inner)
        def _():
            near_copy(c, end).start()

        @pl.when(outer)
        def _():
            near_copy(c, tall).start()

        @pl.when(half == 1)
        def _():
            send_far()

        def own(k, carry):
            risen[c][0, k] = landed[c][table[1, z * tall + k]]
            return carry
        lax.fori_loop(0, tall, own, 0, unroll=4)

    def hand_on(c, place):
        @pl.when(inner)
        def _():
            far_copy(c, place).wait_recv()

            def onward(k, carry):
                passed[c][place, k] = crossed[place][c][jnp.minimum(skip + k, far - 1)]
                return carry
            lax.fori_loop(0, end, onward, 0, unroll=4)
            pass_copy(c, place).start()

            def land(k, carry):
                risen[c][2 + place, k] = crossed[place][c][k]
                return carry
            lax.fori_loop(0, tall, land, 0, unroll=4)

    def hand_on_inner(c):
        hand_on(c, 0)

    def hand_on_outer(c):
        hand_on(c, 1)

    def send_sides(c):
        @pl.when(inner)
        def _():
            near_copy(c, tall).wait_recv()

        @pl.when(outer)
        def _():
            near_copy(c, end).wait_recv()
            pltpu.make_async_copy(passed[c], passed[c], pass_recv.at[c]).wait()

        for d in range(2):
            def leave(k, carry, d=d):
                at = table[2, (d * rows + z) * extra + k]
                for o in range(rows):
                    leaving[c][d, o, k] = risen[c][o, at]
                return carry
            lax.fori_loop(0, extra, leave, 0)
            side_copy(c, d).start()

    def settle(c):
        pltpu.make_async_copy(visiting[c], visiting[c], side_recv.at[c]).wait()
        for r, _ in chunks[c]:
            if max(unit_at[r, t][0] for t in range(times)) == c:
                settle_strip(r)

    def settle_strip(r):
        span = pl.ds(pl.multiple_of(half * (side // 2) + r * PART, PART), PART)

        def place(s, carry):
            for core in (1 - half, half):
                at = table[3, (core * rows + z) * cap + s]
                live = s < table[5, core * rows + z]
                guest = jnp.maximum(at - tall, 0)
                way = guest // extra
                tiles = {}
                for t in range(times):
                    c, i = unit_at[r, t]
                    for o in range(rows):
                        home = risen[c][o, jnp.minimum(at, tall - 1), i]
                        visitor = visiting[c][way, o, guest - way * extra, i]
                        tiles[o, t] = jnp.where(at < tall, home, visitor)
                mean = sum(tiles.values()) * jnp.float32(1.0 / (rows * times))
                for (o, t), tile in tiles.items():
                    value = jnp.where(live, tile - mean, 0.0)
                    if core is half:
                        regional[origin_of(z, rows, o, True) * times + t, 0, s, span, :] = value
                    else:
                        given[r, origin_of(z, rows, o, True) * times + t, s] = value
            return carry
        lax.fori_loop(0, cap, place, 0)
        give = pltpu.make_async_remote_copy(
            src_ref=given.at[r], dst_ref=regional.at[:, 0, :, span, :],
            send_sem=give_send.at[0], recv_sem=give_recv.at[0], device_id=mate, device_id_type=MESH)
        give.start()

    starts = []
    for chunk in chunks:
        begin = starts[-1][1] if starts else 0
        starts.append((begin, begin + len(chunk)))
    for _, _, c, act in timetable(starts, wide, tall, end, far, extra, (send_pairs, send_rows, hand_on_outer, hand_on_inner, send_sides, settle)):
        act(c)

    wait_sent(swap_send.at[0], per_group)
    for o in range(1, pairs):
        wait_sent(pair_send.at[o - 1], wide)
    wait_sent(far_send.at[0], far)
    wait_sent(side_send.at[0], 2 * rows * extra)

    @pl.when(inner)
    def _():
        wait_sent(near_send.at[0], end)
        wait_sent(pass_send.at[0], 2 * end)

    @pl.when(outer)
    def _():
        wait_sent(near_send.at[0], tall)

    wait_sent(give_send.at[0], rows * cap)
    wait_sent(give_recv.at[0], rows * cap)


def timetable(starts, wide, tall, end, far, extra, acts):
    hop = 60
    sent = soon = crossed = passed = 0.0
    busy = 4 * wide * starts[-1][1]
    events = []
    for c, (begin, close) in enumerate(starts):
        size = close - begin
        sent = sent + 4 * wide * size
        landed = sent + hop
        soon = max(soon, landed) + 1.9 * (tall + far) * size
        crossed = max(crossed, landed) + 4 * far * size
        passed = max(passed, crossed + hop) + 4 * end * size
        sides = passed + hop
        busy = max(busy, sides) + 8 * extra * size
        for k, at in enumerate((0.0, landed, soon + hop, crossed + hop, sides, busy + 2 * hop)):
            events.append((at, k, c, acts[k]))
    return sorted(events, key=lambda e: e[:3])


def on_device(field, zone, slot, spins, tally):
    times, per_group, side, _ = field.shape
    columns = lax.axis_size("gx")
    rows = lax.axis_size("gy")
    pairs = columns // 2
    cap = 2 * per_group // rows
    per_pair = 4 * (2 * per_group // columns)
    balanced = rows == 4 and pairs == 4 and times == 2 and columns * per_group < 256 and 2 * rows * cap <= 128 and pairs * per_pair <= 128
    if balanced:
        return balanced_exchange(field, zone, slot, spins, cap, per_pair)
    chunks = chunk_units(times, side)
    tiles = [(len(chunk), PART, side) for chunk in chunks]
    final = plain_exchange(field, zone, slot, spins, chunks, tiles, cap, per_pair)
    return pl.pallas_call(
        functools.partial(finish, rows, chunks),
        grid_spec=pltpu.PrefetchScalarGridSpec(
            num_scalar_prefetch=1,
            grid=(cap,),
            in_specs=[pl.BlockSpec(
                (2, 1, rows) + tile,
                lambda s, count: (0, jnp.maximum(jnp.minimum(s, count[0] - 1), 0), 0, 0, 0, 0)) for tile in tiles],
            out_specs=pl.BlockSpec((rows * times, 1, 1, side, side), lambda s, count: (0, 0, s, 0, 0)),
        ),
        out_shape=jax.ShapeDtypeStruct((rows * times, 1, cap, side, side), jnp.float32),
        name="finish",
    )(tally, *final)


def scratch_of(tiles, *shapes):
    return [pltpu.VMEM(lead + tile, jnp.float32) for lead in shapes for tile in tiles]


def balanced_exchange(field, zone, slot, spins, cap, per_pair):
    times, per_group, side, _ = field.shape
    columns = lax.axis_size("gx")
    rows = lax.axis_size("gy")
    pairs = columns // 2
    tall = 2 * cap
    extra = cap // 3
    chunks = time_major(times, side)
    tiles = [(len(chunk), PART, side) for chunk in chunks]
    count = len(chunks)
    strips = side // (2 * PART)
    smem = pl.BlockSpec(memory_space=pltpu.SMEM)
    vmem = pl.BlockSpec(memory_space=pltpu.VMEM)
    sizes = balanced_sizes(per_pair, tall)
    lanes = -(-columns * per_group // 128) * 128
    table, choice = pl.pallas_call(
        functools.partial(prepare_balanced, (pairs, rows, per_group, per_pair, cap, extra), sizes),
        in_specs=[vmem, vmem],
        out_specs=[vmem, smem],
        out_shape=[jax.ShapeDtypeStruct((8, 128), jnp.int32), jax.ShapeDtypeStruct((1,), jnp.int32)],
        scratch_shapes=[pltpu.VMEM((8, lanes), jnp.int32)],
        name="prepare",
    )(zone.reshape(1, -1), slot.reshape(1, -1))

    def moved(wide, end, far, tag):
        dma = pltpu.SemaphoreType.DMA
        buffers = [
            *scratch_of(
                tiles, (2 * per_group,), (per_group,), (pairs - 1, wide), (pairs * per_pair,), (tall,), (rows, tall),
                (far,), (far,), (far,), (2, end), (2, rows, extra), (2, rows, extra)),
            pltpu.VMEM((max(times * per_group, rows * cap, 2 * end, far), side, side), jnp.float32),
            pltpu.VMEM((strips, rows * times, cap, PART, side), jnp.float32),
            pltpu.SMEM((far,), jnp.int32),
            dma((times,)), dma((1,)), dma((count,)), dma((pairs - 1,)), dma((count,)), dma((1,)), dma((count,)),
            dma((1,)), dma((1,)), dma((1,)), dma((count, 2)), dma((1,)), dma((count,)), dma((1,)), dma((count,)),
        ]
        return lambda: pl.pallas_call(
            functools.partial(
                exchange_balanced, (pairs, rows, per_group, per_pair, cap, extra, wide, end, far), chunks),
            in_specs=[smem, smem, pl.BlockSpec(memory_space=pl.ANY)],
            out_specs=vmem,
            out_shape=pltpu.VMEM((rows * times, 1, cap, side, side), jnp.float32),
            scratch_shapes=buffers,
            compiler_params=pltpu.CompilerParams(collective_id=tag, has_side_effects=True, vmem_limit_bytes=VMEM_BYTES),
            name=f"exchange_{tag}",
        )(table, spins, field)

    return lax.switch(choice[0], [moved(*size, tag) for tag, size in enumerate(sizes)])


def plain_exchange(field, zone, slot, spins, chunks, tiles, cap, per_pair):
    times, per_group, side, _ = field.shape
    columns = lax.axis_size("gx")
    rows = lax.axis_size("gy")
    pairs = columns // 2
    per_row = 2 * cap
    smem = pl.BlockSpec(memory_space=pltpu.SMEM)
    anywhere = pl.BlockSpec(memory_space=pl.ANY)
    i32 = jnp.int32
    narrow = levels(per_pair, (40,))[0]
    sizes = [(narrow, tall) for tall in levels(per_row, (36, 42))]
    sizes.append((per_pair, per_row))
    *turned, send_table, pick_table, tallies, choice = pl.pallas_call(
        functools.partial(prepare, (pairs, rows, per_group, per_pair, cap, chunks, sizes)),
        grid=(per_group // STEP_BLOCKS,),
        in_specs=[smem, smem, smem, pl.BlockSpec((times, STEP_BLOCKS, side, side), lambda i: (0, i, 0, 0))],
        out_specs=[
            *[pl.BlockSpec((2, STEP_BLOCKS) + tile, lambda i: (0, i, 0, 0, 0)) for tile in tiles],
            smem, smem, smem, smem,
        ],
        out_shape=[
            *[jax.ShapeDtypeStruct((2, per_group) + tile, jnp.float32) for tile in tiles],
            jax.ShapeDtypeStruct((pairs * per_pair + 1,), i32),
            jax.ShapeDtypeStruct((per_row * rows + 1,), i32),
            jax.ShapeDtypeStruct((2 * rows,), i32),
            jax.ShapeDtypeStruct((1,), i32),
        ],
        scratch_shapes=[pltpu.SMEM((columns * rows,), i32), pltpu.SMEM((pairs * pairs,), i32)],
        name="prepare",
    )(zone, slot, spins, field)
    count = len(chunks)

    def moved(wide, tall, tag):
        dma = pltpu.SemaphoreType.DMA
        buffers = [
            *scratch_of(
                tiles, (2 * per_group,), (pairs - 1, wide), (pairs * per_pair,), (rows - 1, tall), (rows, tall),
                (cap, rows), (cap, rows)),
            pltpu.SMEM((rows * tall,), i32),
            dma((count,)), dma((count,)), dma((count,)),
            dma((count, pairs - 1)), dma((count, pairs - 1)),
            dma((count, rows - 1)), dma((count, rows - 1)),
            dma((count,)), dma((count,)), dma((count,)),
        ]
        return lambda: pl.pallas_call(
            functools.partial(exchange, (pairs, rows, per_group, per_pair, wide, tall, cap, count)),
            in_specs=[smem, smem, smem] + [anywhere] * count,
            out_specs=[anywhere] * count,
            out_shape=[jax.ShapeDtypeStruct((2, cap, rows) + tile, jnp.float32) for tile in tiles],
            scratch_shapes=buffers,
            compiler_params=pltpu.CompilerParams(collective_id=tag, has_side_effects=True, vmem_limit_bytes=60 * 2**20),
            name=f"exchange_{tag}",
        )(send_table, pick_table, tallies, *turned)

    return lax.switch(choice[0], [moved(*size, tag) for tag, size in enumerate(sizes)])


def solution(mesh):
    placed = (P("gy", "gx", None, None), P(), P(), P(), P(("gx", "gy")))
    return jax.shard_map(
        on_device,
        mesh=mesh,
        in_specs=placed,
        out_specs=P(None, ("gx", "gy"), None, None, None),
        check_vma=False,
    )
```

profile of v0, /device:TPU:0, one launch (start us, length us, event | category | flops | bytes accessed | tf_op | source)
XLA Modules:
  0.0 106.1 jit_solution(4961709240069739665)
XLA Ops:
  0.0 1.9 %prepare.1 = (s32[8,128]{1,0:T(8,128)S(1)}, s32[1]{0:T(128)}) custom-call(s32[1,192]{1,0:T(1,128)} %bitcast.3, s32[1,192]{1,0:T(1,128)} %bitcast.4), custom_call_target="tpu_custom_call" | custom-call | tf_op jit(solution)/shard_map/prepare/pallas_call | solution.py:801
  2.6 100.8 %conditional.1 = (f32[8,1,12,128,128]{4,3,2,1,0:T(8,128)S(1)}) conditional(s32[]{:T(128)} %bitcast.2, (s32[8,128]{1,0:T(8,128)S(1)}, s32[192]{0:T(256)}, f32[2,24,128,128]{3,2,1,0:T(8,128)}) %tuple.26, (s32[8,128]{1,0:T(8,128)S(1)}, s32[192]{0:T(256)}, f32[2,24,128,128]{3,2,1,0:T(8,128)}) %tuple.26, ...), branch_computations={%region_0.0_spmd, %region_1.0_spmd, %region_2.0_spmd, %region_3.0_... | conditional | bytes 8 | solution.py:833
  2.6 100.6 %exchange_0.1 = f32[8,1,12,128,128]{4,3,2,1,0:T(8,128)S(1)} custom-call(s32[8,128]{1,0:T(8,128)S(1)} %get-tuple-element.49.table, s32[192]{0:T(256)} %get-tuple-element.50.spins, f32[2,24,128,128]{3,2,1,0:T(8,128)} %get-tuple-element.51.field), custom_call_target="tpu_custom_call" | custom-call | tf_op jit(solution)/shard_map/cond/branch_0_fun/exchange_0/pallas_call | solution.py:822
  103.4 2.7 %copy.20 = f32[8,1,12,128,128]{4,3,2,1,0:T(8,128)} copy(f32[8,1,12,128,128]{4,3,2,1,0:T(8,128)S(1)} %get-tuple-element.80) | data formatting | bytes 12582912
where the time goes:
time: 107 us; the launch traced here: 106 us
  Pallas kernels  102 us (95%)
  local copies, waits for them, and re-layouts  2.71 us (3%)
    pallas_call x1, Pallas kernels, moved(): pl.pallas_call(functools.partial(exchange_balanced, (pairs, rows, per_gro...  101 us
    unnamed x1, local copies, waits for them, and re-layouts  2.71 us

commit v1 on v0

--- a/solution.py
+++ b/solution.py
@@ -290,7 +290,9 @@
 
 
 def balanced_sizes(per_pair, tall):
-    steps = ((38, 34, 52), (38, 36, 54), (40, 36, 56), (40, 38, 58), (42, 40, 60), (48, 46, 68), (48, 48, 96))
+    steps = (
+        (36, 34, 52), (36, 36, 54), (38, 36, 56), (42, 38, 56), (38, 38, 58), (40, 40, 60), (44, 44, 64), (48, 48, 70),
+        (48, 48, 96))
     return [(-(-per_pair * w // 48), -(-tall * e // 48), -(-tall * f // 48)) for w, e, f in steps]
 
 def beside(x, step):
@@ -325,22 +327,31 @@
     def ranks(mark):
         return jnp.dot(mark.astype(bf16), before, preferred_element_type=f32)
 
-    at = lax.broadcasted_iota(i32, (bins, 128), 0)
-    at_row = at & (rows - 1)
-    at_home = at >> (rows.bit_length() - 1)
+    spot = lax.broadcasted_iota(i32, (bins, 128), 0)
+    at_row = spot & (rows - 1)
+    at_home = spot >> (rows.bit_length() - 1)
     edge = jnp.logical_or(at_row == 0, at_row == rows - 1)
 
     def flip(x, bit):
         step = 1 << bit
         if 2 * step == bins:
             return beside(x, step)
-        return jnp.where((at & step) == 0, beside(x, step), beside(x, bins - step))
+        return jnp.where((spot & step) == 0, beside(x, step), beside(x, bins - step))
 
     across_x = lambda x: flip(x, 2)
     across_y = lambda x: flip(x, 3)
     mark = marks(home * rows + row)
-    order = look(mark, ranks(mark))
-    native = jnp.broadcast_to(tally(mark), (bins, 128)).astype(i32)
+    home_x = home & 1
+    home_y = home >> 1
+    beside_x = home_y * 2 + 1 - home_x
+    beside_y = (1 - home_y) * 2 + home_x
+    kinds = [source == beside_x, jnp.logical_and(source != beside_x, source != beside_y), source == beside_y]
+    split = [jnp.where(kind, mark, 0.0) for kind in kinds]
+    split_ranks = ranks(jnp.concatenate(split, axis=0))
+    counts = [tally(part) for part in split]
+    order = sum(look(part, split_ranks[k * bins:(k + 1) * bins] + sum(counts[:k])) for k, part in enumerate(split))
+    total = sum(counts)
+    native = jnp.broadcast_to(total, (bins, 128)).astype(i32)
 
     def whole(x):
         x = x + across_x(x)
@@ -365,12 +376,11 @@
     first = look(mark, (used[0] * allow)[:, :1].astype(f32))
     second = look(mark, (used[1] * allow)[:, :1].astype(f32))
     leaves_x = order < first
-    leaves_y = jnp.logical_and(order >= first, order < first + second)
+    keeps = look(mark, total) - second
+    leaves_y = order >= keeps
     way = leaves_y.astype(i32)
-    guest = order - jnp.where(leaves_y, first, 0.0)
-    home_x = home & 1
-    home_y = home >> 1
-    via = jnp.where(leaves_x, home_y * 2 + 1 - home_x, jnp.where(leaves_y, (1 - home_y) * 2 + home_x, home))
+    guest = order - jnp.where(leaves_y, keeps, 0.0)
+    via = jnp.where(leaves_x, beside_x, jnp.where(leaves_y, beside_y, home))
 
     flow = marks(source * pairs + via)
     line = marks(via * rows + row)
@@ -381,12 +391,12 @@
     lines = jnp.broadcast_to(tally(line), (bins, 128))
     halves = lines + flip(lines, 0)
     stays = at_home == at_row
-    chosen = jnp.zeros((1, 128), f32)
-    for wide, end, far in sizes:
-        over = jnp.where(flows > jnp.where(stays, per_pair, wide).astype(f32), 1.0, 0.0)
+    chosen = jnp.full((1, 128), len(sizes), i32)
+    for at, (wide, end, far) in reversed(list(enumerate(sizes))):
+        over = jnp.where(flows > jnp.where(stays, per_pair + 2 * extra, wide).astype(f32), 1.0, 0.0)
         over = jnp.maximum(over, jnp.where(lines > jnp.where(edge, end, tall).astype(f32), 1.0, 0.0))
         over = jnp.maximum(over, jnp.where(halves > jnp.float32(far), 1.0, 0.0))
-        chosen = chosen + jnp.max(over, axis=0, keepdims=True)
+        chosen = jnp.where(jnp.max(over, axis=0, keepdims=True) > 0.0, chosen, at)
 
     my_x, my_y = pair % 2, pair // 2
 
@@ -404,11 +414,15 @@
     rank = rank.astype(i32)
     place = place.astype(i32)
     guest = guest.astype(i32)
-    landing = offset(source) * per_pair + rank
+
+    def based(hop):
+        return hop * per_pair + jnp.where(hop > 0, 2 * extra, 0)
+
+    landing = based(offset(source)) + rank
     mine = via == pair
     ours = home == pair
     return chosen, [
-        invert(source == pair, offset(via) * per_pair + rank, (lane - group * pair).astype(f32)),
+        invert(source == pair, based(offset(via)) + rank, (lane - group * pair).astype(f32)),
         invert(mine, row * tall + place, landing.astype(f32)),
         invert(jnp.logical_and(mine, home != pair), (way * rows + row) * extra + guest, place.astype(f32)),
         invert(ours, (side * rows + row) * cap + slot, jnp.where(mine, place, tall + way * extra + guest).astype(f32)),
@@ -427,7 +441,7 @@
         chosen, lines = plan_tables(dims, sizes, pair, padded[0:1], padded[1:2], allow)
         for k, line in enumerate(lines):
             table[k:k + 1] = line.astype(jnp.int32)
-        return jnp.max(chosen).astype(jnp.int32)
+        return jnp.max(chosen)
 
     chosen = fill(sizes, 1)
     choice[0] = jnp.minimum(chosen, len(sizes) - 1)
@@ -531,11 +545,11 @@
         sent = []
         for o in range(1, pairs):
             def pack(k, carry, o=o):
-                packed[c][o - 1, k] = held[c][table[0, o * per_pair + k]]
+                packed[c][o - 1, k] = held[c][table[0, o * per_pair + 2 * extra + k]]
                 return carry
             lax.fori_loop(0, wide, pack, 0, unroll=4)
             sent.append(pltpu.make_async_remote_copy(
-                src_ref=packed[c].at[o - 1], dst_ref=landed[c].at[pl.ds(o * per_pair, wide)],
+                src_ref=packed[c].at[o - 1], dst_ref=landed[c].at[pl.ds(o * per_pair + 2 * extra, wide)],
                 send_sem=pair_send.at[o - 1], recv_sem=pair_recv.at[c],
                 device_id=across(o), device_id_type=MESH))
 
@@ -552,7 +566,7 @@
         def stay(k, carry):
             landed[c][k] = held[c][table[0, k]]
             return carry
-        lax.fori_loop(0, per_pair, stay, 0, unroll=4)
+        lax.fori_loop(0, per_pair + 2 * extra, stay, 0, unroll=4)
 
         if c == 0:
             lead = table[4, far_in]
@@ -741,7 +755,7 @@
         size = close - begin
         sent = sent + 4 * wide * size
         landed = sent + hop
-        soon = max(soon, landed) + 1.9 * (tall + far) * size
+        soon = max(soon, landed) + 1.95 * (tall + far) * size
         crossed = max(crossed, landed) + 4 * far * size
         passed = max(passed, crossed + hop) + 4 * end * size
         sides = passed + hop
@@ -758,7 +772,7 @@
     pairs = columns // 2
     cap = 2 * per_group // rows
     per_pair = 4 * (2 * per_group // columns)
-    balanced = rows == 4 and pairs == 4 and times == 2 and columns * per_group < 256 and 2 * rows * cap <= 128 and pairs * per_pair <= 128
+    balanced = rows == 4 and pairs == 4 and times == 2 and columns * per_group < 256 and 2 * rows * cap <= 128 and pairs * per_pair + 2 * (cap // 3) <= 128
     if balanced:
         return balanced_exchange(field, zone, slot, spins, cap, per_pair)
     chunks = chunk_units(times, side)
@@ -811,7 +825,7 @@
         dma = pltpu.SemaphoreType.DMA
         buffers = [
             *scratch_of(
-                tiles, (2 * per_group,), (per_group,), (pairs - 1, wide), (pairs * per_pair,), (tall,), (rows, tall),
+                tiles, (2 * per_group,), (per_group,), (pairs - 1, wide), (pairs * per_pair + 2 * extra,), (tall,), (rows, tall),
                 (far,), (far,), (far,), (2, end), (2, rows, extra), (2, rows, extra)),
             pltpu.VMEM((max(times * per_group, rows * cap, 2 * end, far), side, side), jnp.float32),
             pltpu.VMEM((strips, rows * times, cap, PART, side), jnp.float32),

time: 107 us -> 107 us (level); the launches traced: 106 us -> 107 us
  no operation moved by 1% of the time
where the time goes in v1:
time: 107 us
  Pallas kernels  103 us (96%)
  local copies, waits for them, and re-layouts  2.71 us (3%)
    pallas_call x1, Pallas kernels, moved(): pl.pallas_call(functools.partial(exchange_balanced, (pairs, rows, per_gro...  101 us
    unnamed x1, local copies, waits for them, and re-layouts  2.71 us

profile of v1, /device:TPU:0, one launch (start us, length us, event | category | flops | bytes accessed | tf_op | source)
XLA Modules:
  0.0 107.2 jit_solution(9653953350906996871)
XLA Ops:
  0.0 1.9 %prepare.1 = (s32[8,128]{1,0:T(8,128)S(1)}, s32[1]{0:T(128)}) custom-call(s32[1,192]{1,0:T(1,128)} %bitcast.3, s32[1,192]{1,0:T(1,128)} %bitcast.4), custom_call_target="tpu_custom_call" | custom-call | tf_op jit(solution)/shard_map/prepare/pallas_call | solution.py:815
  2.6 101.9 %conditional.1 = (f32[8,1,12,128,128]{4,3,2,1,0:T(8,128)S(1)}) conditional(s32[]{:T(128)} %bitcast.2, (s32[8,128]{1,0:T(8,128)S(1)}, s32[192]{0:T(256)}, f32[2,24,128,128]{3,2,1,0:T(8,128)}) %tuple.32, (s32[8,128]{1,0:T(8,128)S(1)}, s32[192]{0:T(256)}, f32[2,24,128,128]{3,2,1,0:T(8,128)}) %tuple.32, ...), branch_computations={%region_0.0_spmd, %region_1.0_spmd, %region_2.0_spmd, %region_3.0_... | conditional | bytes 8 | solution.py:847
  2.6 101.4 %exchange_1.1 = f32[8,1,12,128,128]{4,3,2,1,0:T(8,128)S(1)} custom-call(s32[8,128]{1,0:T(8,128)S(1)} %get-tuple-element.66.table, s32[192]{0:T(256)} %get-tuple-element.67.spins, f32[2,24,128,128]{3,2,1,0:T(8,128)} %get-tuple-element.72.field), custom_call_target="tpu_custom_call" | custom-call | tf_op jit(solution)/shard_map/cond/branch_1_fun/exchange_1/pallas_call | solution.py:836
  104.5 2.7 %copy.24 = f32[8,1,12,128,128]{4,3,2,1,0:T(8,128)} copy(f32[8,1,12,128,128]{4,3,2,1,0:T(8,128)S(1)} %get-tuple-element.100) | data formatting | bytes 12582912
